TPU v7x, 16 devices: a whole 2x2x2 slice. The times are simulated.
16 devices in a mesh: outer: 2 (over z), inner: 8 (over y, x, core).
Axes of the slice: x: 2, y: 2, z: 2, core: 2. Of those that a mesh axis runs over, the one named last changes fastest.
Arguments:
- g_emb: float32 [16, 4096, 1024], P(('outer', 'inner'))
- g_qkv: float32 [16, 1, 1024, 3072], P(('outer', 'inner'))
- g_o: float32 [16, 1, 1024, 1024], P(('outer', 'inner'))
- g_w1: float32 [16, 1, 1024, 2816], P(('outer', 'inner'))
- g_w2: float32 [16, 1, 2816, 1024], P(('outer', 'inner'))
- g_bqkv: float32 [16, 1, 3072], P(('outer', 'inner'))
- g_b1: float32 [16, 1, 2816], P(('outer', 'inner'))
- g_dvec: float32 [16, 1, 6, 1024], P(('outer', 'inner'))
- m: float32 [14167808], P(('outer', 'inner'))
- v: float32 [14167808], P(('outer', 'inner'))
- w: float32 [14167808], P(('outer', 'inner'))
- lr: float32 [], replicated
- beta1: float32 [], replicated
- beta2: float32 [], replicated
- eps: float32 [], replicated
- step: int32 [], replicated
Outputs:
- output 1: float32 [14167808], P(('outer', 'inner'))
- output 2: float32 [14167808], P(('outer', 'inner'))
- output 3: float32 [14167808], P(('outer', 'inner'))
- output 4: bfloat16 [4096, 1024], replicated
- output 5: bfloat16 [1, 1024, 3072], replicated
- output 6: bfloat16 [1, 1024, 1024], replicated
- output 7: bfloat16 [1, 1024, 2816], replicated
- output 8: bfloat16 [1, 2816, 1024], replicated
- output 9: bfloat16 [1, 3072], replicated
- output 10: bfloat16 [1, 2816], replicated
- output 11: bfloat16 [1, 6, 1024], replicated
All inputs are finite; a program needn't handle non-finite values.
Results may differ from a plain program's by a relative error of at most 0.001.
Values are sent between devices in bfloat16 or wider.
A program may use at most 1 GiB of HBM per device.

v0:
```python
import functools
import math
import jax
import jax.numpy as jnp
from jax import lax
from jax.experimental import pallas as pl
from jax.experimental.pallas import tpu as pltpu
from jax.sharding import PartitionSpec as P

AXES = ("outer", "inner")
MESH = pl.DeviceIdType.MESH
F32, BF16 = jnp.float32, jnp.bfloat16
NDEV = 16
SHARD = 885488
BIG = ((4096, 1024), (1024, 3072), (1024, 1024), (1024, 2816), (2816, 1024))
PER = tuple(c // 128 for _, c in BIG) + (1,)
SMALL = (3072, 2816, 6144)
SMALL_TILES = 32
TOFF = [0]
for _r, _c in BIG:
    TOFF.append(TOFF[-1] + _r * _c // 1024)
TOFF.append(TOFF[-1] + SMALL_TILES)
NBLK = tuple((TOFF[k + 1] - TOFF[k]) // PER[k] for k in range(6))

WIN = 888
SUB = 148
CH = SUB * 8
WR = WIN * 8
PIECE = 4
COLORS = ((1, 2, 3), (2, 3, 1), (3, 1, 2))


def win_start(w):
    def ge(t):
        return (w + 16 - t) // 16
    return 864 * w + 8 * (ge(9) - ge(5) - ge(10) + 2 * ge(11) - ge(12) + ge(13))


def block_start(w):
    e = w * SHARD
    t = e // 1024
    k = max(i for i in range(6) if TOFF[i] <= t)
    n = PER[k]
    return TOFF[k] + ((e - TOFF[k] * 1024) // (n * 1024)) * n, n, k


def my_id():
    return lax.axis_index("outer") * 8 + lax.axis_index("inner")


def coords(d):
    return (d // 8, d % 8)


def deltas(me):
    return [(1 - 2 * ((me // (1 << d)) % 2)) * (1 << d) for d in range(4)]


def entry_barrier(peers):
    sem = pltpu.get_barrier_semaphore()
    for p in peers:
        pl.semaphore_signal(sem, inc=1, device_id=p, device_id_type=MESH)
    pl.semaphore_wait(sem, 4)


BLK = 4096
NB = SHARD // BLK
TAIL = SHARD % BLK // 128
LAST = SHARD % 128
PAD = 200


NST = 6


def step_kernel(sc, g0, g1, g2, g3, g4, g5, m_in, v_in, w_in, out, m_out, v_out, w_out,
                acc, r1, r2, r3, stage, raw, mine,
                dsend, drecv, own, s1, q1, s2, q2, s3, q3, lsem, isend, irecv, asend, arecv):
    grads = (g0, g1, g2, g3, g4, g5)
    me = my_id()
    delta = deltas(me)
    peers = [coords(me + x) for x in delta]
    entry_barrier(peers)
    partner = peers[0]

    def from_grads(start, go):
        for k in range(6):
            @pl.when((start >= TOFF[k]) & (start + SUB <= TOFF[k + 1]))
            def _(k=k):
                go(grads[k].at[pl.ds(pl.multiple_of((start - TOFF[k]) * 8, 32), CH)], 0, CH)
        for k in range(1, 6):
            @pl.when((start < TOFF[k]) & (start + SUB > TOFF[k]))
            def _(k=k):
                def body(j, _):
                    @pl.when(start + j * PIECE < TOFF[k])
                    def _():
                        go(grads[k - 1].at[pl.ds(pl.multiple_of((start + j * PIECE - TOFF[k - 1]) * 8, 32), PIECE * 8)],
                           j * PIECE * 8, PIECE * 8)

                    @pl.when(start + j * PIECE >= TOFF[k])
                    def _():
                        go(grads[k].at[pl.ds(pl.multiple_of((start + j * PIECE - TOFF[k]) * 8, 32), PIECE * 8)],
                           j * PIECE * 8, PIECE * 8)
                    return 0
                lax.fori_loop(0, SUB // PIECE, body, 0)

    def chunk(ref, i):
        return ref.at[pl.ds(pl.multiple_of(i * CH, CH), CH)]

    def tile_of(n, k, core):
        half = 1 - n // 8
        i = n % 8
        j = i // 2
        d1, d2, d3 = COLORS[k]
        w = me + core * delta[0] + half * delta[d1] + (1 - j // 2) * delta[d2] + (1 - j % 2) * delta[d3]
        return win_start(w) + (2 * k + i % 2) * SUB

    def d2d_start(n):
        for k in range(3):
            c = n * 3 + k

            def go(src, off, rows, c=c):
                pltpu.make_async_remote_copy(
                    src, acc.at[pl.ds(pl.multiple_of(c * CH + off, 32), rows)], dsend.at[c], drecv.at[c],
                    device_id=partner, device_id_type=MESH).start()
            from_grads(tile_of(n, k, 1), go)

    def own_start(n):
        for k in range(3):
            slot = (n % 2) * 3 + k

            def go(src, off, rows, slot=slot):
                pltpu.make_async_copy(src, stage.at[pl.ds(pl.multiple_of(slot * CH + off, 32), rows)], own.at[slot]).start()
            from_grads(tile_of(n, k, 0), go)

    def add(dst, i, srcs):
        def body(t, _):
            o = t * 32
            x = dst[pl.ds(pl.multiple_of(i * CH + o, 32), 32), :]
            for ref, s in srcs:
                x = x + ref[pl.ds(pl.multiple_of(s * CH + o, 32), 32), :]
            dst[pl.ds(pl.multiple_of(i * CH + o, 32), 32), :] = x
            return 0
        lax.fori_loop(0, CH // 32, body, 0)

    def hop(src, i, dst, j, ssem, rsem, k, step):
        return pltpu.make_async_remote_copy(
            chunk(src, i), chunk(dst, j), ssem.at[j], rsem.at[j],
            device_id=peers[COLORS[k][step]], device_id_type=MESH)

    def d2d_desc(c):
        return pltpu.make_async_remote_copy(chunk(acc, c), chunk(acc, c), dsend.at[c], drecv.at[c],
                                            device_id=partner, device_id_type=MESH)

    AHEAD = 4
    own_start(0)
    for n in range(AHEAD):
        d2d_start(n)
        if n == 0:
            own_start(1)

    def first(n, _):
        @pl.when(n + AHEAD < 16)
        def _():
            d2d_start(n + AHEAD)
        for k in range(3):
            c = n * 3 + k
            slot = (n % 2) * 3 + k
            pltpu.make_async_copy(chunk(stage, slot), chunk(stage, slot), own.at[slot]).wait()
            d2d_desc(c).wait_recv()
            add(acc, c, ((stage, slot),))

            @pl.when(n < 8)
            def _():
                hop(acc, c, r1, c, s1, q1, k, 0).start()

        @pl.when(n + 2 < 16)
        def _():
            own_start(n + 2)
        return 0
    lax.fori_loop(0, 16, first, 0)

    def second(i, _):
        for k in range(3):
            c = i * 3 + k
            hop(acc, c, r1, c, s1, q1, k, 0).wait_recv()
            add(acc, 24 + c, ((r1, c),))
            hop(acc, 24 + c, r2, c, s2, q2, k, 1).start()
        return 0
    lax.fori_loop(0, 4, second, 0)

    start = me * SHARD
    off = start % 128
    base = win_start(me)
    q = (start - off) // 128 - 8 * base
    flat_rows = acc
    lane8 = lax.broadcasted_iota(jnp.int32, (8, 128), 1)

    def each_block(one):
        for k in range(6):
            n = PER[k]
            e0 = start - TOFF[k] * 1024
            lo = jnp.minimum(jnp.maximum(e0, 0) // (n * 1024), NBLK[k])
            hi = jnp.minimum((jnp.maximum(e0 + SHARD, 0) + n * 1024 - 1) // (n * 1024), NBLK[k])
            t0 = TOFF[k] - base

            def body(b, _, t0=t0, n=n):
                row = pl.multiple_of((t0 + b * n) * 8, 8)
                if n == 22:
                    @pl.when(row + 8 * n <= WR)
                    def _():
                        one(row, n, n)

                    @pl.when(row + 8 * n > WR)
                    def _():
                        one(row, n, 8)
                else:
                    one(row, n, n)
                return 0
            lax.fori_loop(lo, hi, body, 0)

    def pieces(one):
        def body(i, _):
            one(pl.multiple_of(i * (BLK // 128), 8), BLK // 128, 128, pl.multiple_of(i * BLK, BLK))
            return 0
        lax.fori_loop(0, NB, body, 0)
        one(NB * BLK // 128, TAIL, 128, NB * BLK)
        one(NB * BLK // 128 + TAIL, 1, LAST, NB * BLK + TAIL * 128)

    def to_tile_order(src, dst, first):
        load = pltpu.make_async_copy(src, raw, lsem.at[0])
        load.start()
        load.wait()

        def shift(row, rows, cols, e):
            x = raw[pl.ds(e, rows * cols)].reshape(rows, cols)
            if cols < 128:
                x = jnp.concatenate([x, jnp.zeros((rows, 128 - cols), F32)], axis=1)
            flat_rows[pl.ds(row + PAD, rows), :] = pltpu.roll(x, off, 1)
        pieces(shift)

        def block(row, n, todo):
            for j in range(todo):
                x = flat_rows[pl.ds(row + j - q + PAD, 8, stride=n), :]
                y = flat_rows[pl.ds(row + j - q + PAD - 1, 8, stride=n), :]
                dst[pl.ds(pl.multiple_of(first + row + 8 * j, 8), 8), :] = jnp.where(lane8 >= off, x, y)
        each_block(block)

    def to_flat_order(src, first, dst):
        def block(row, n, todo):
            for j in range(todo):
                flat_rows[pl.ds(row + j, 8, stride=n), :] = src[pl.ds(pl.multiple_of(first + row + 8 * j, 8), 8), :]
        each_block(block)
        back = (128 - off) % 128

        def shift(row, rows, cols, e):
            lane = lax.broadcasted_iota(jnp.int32, (rows, 128), 1)
            x = pltpu.roll(flat_rows[pl.ds(q + row, rows), :], back, 1)
            y = pltpu.roll(flat_rows[pl.ds(q + row + 1, rows), :], back, 1)
            raw[pl.ds(e, rows * cols)] = jnp.where(lane < 128 - off, x, y)[:, :cols].reshape(rows * cols)
        pieces(shift)
        store = pltpu.make_async_copy(raw, dst, lsem.at[0])
        store.start()
        store.wait()

    def free1(i, _):
        for k in range(3):
            hop(acc, i * 3 + k, r1, i * 3 + k, s1, q1, k, 0).wait_send()
        return 0
    lax.fori_loop(0, 4, free1, 0)
    state = ((m_in, m_out, r1, 0), (v_in, v_out, r1, WR), (w_in, w_out, stage, 0))
    for src, _, dst, first in state:
        to_tile_order(src, dst, first)

    def third(i, _):
        for k in range(3):
            c = i * 3 + k
            hop(acc, 12 + c, r1, 12 + c, s1, q1, k, 0).wait_recv()
            hop(acc, c, r2, c, s2, q2, k, 1).wait_recv()
            add(acc, 36 + c, ((r1, 12 + c), (r2, c)))
            hop(acc, 36 + c, r3, c, s3, q3, k, 2).start()
        return 0
    lax.fori_loop(0, 2, third, 0)

    def fourth(i, _):
        for k in range(3):
            c = i * 3 + k
            hop(acc, 18 + c, r1, 18 + c, s1, q1, k, 0).wait_recv()
            hop(acc, 6 + c, r2, 6 + c, s2, q2, k, 1).wait_recv()
            add(acc, 42 + c, ((r1, 18 + c), (r2, 6 + c)))
        return 0
    lax.fori_loop(0, 2, fourth, 0)

    def slot(k, s, e):
        d1, d2, d3 = COLORS[k]
        w = me + (e % 2) * delta[d1] + (e // 2 % 2) * delta[d2] + (e // 4) * delta[d3]
        return out.at[pl.ds(pl.multiple_of(w * WR + (2 * k + s) * CH, 32), CH)]

    def mine_at(k, s):
        return mine.at[pl.ds((2 * k + s) * CH, CH)]

    def send(src, dst, k, s, e, step):
        i = (k * 2 + s) * 8 + e + (1 << step)
        return pltpu.make_async_remote_copy(src, dst, isend.at[i], irecv.at[i],
                                            device_id=peers[COLORS[k][step]], device_id_type=MESH)

    def across(src, dst, k, s, e):
        i = (k * 2 + s) * 8 + e
        return pltpu.make_async_remote_copy(src, dst, asend.at[i], arecv.at[i], device_id=peers[0], device_id_type=MESH)

    lr, b1, b2, eps, ic1, ic2 = (sc[i] for i in range(6))

    def fifth(i, _):
        for k in range(3):
            c = i * 3 + k
            hop(acc, 36 + c, r3, c, s3, q3, k, 2).wait_recv()

            def adam(t, _, c=c, k=k):
                o = t * 32
                g = (acc[pl.ds(pl.multiple_of((42 + c) * CH + o, 32), 32), :]
                     + r3[pl.ds(pl.multiple_of(c * CH + o, 32), 32), :]) * (1.0 / NDEV)
                p = (2 * k + i) * CH + o
                here = pl.ds(pl.multiple_of(p, 32), 32)
                there = pl.ds(pl.multiple_of(WR + p, 32), 32)
                m = b1 * r1[here, :] + (1.0 - b1) * g
                v = b2 * r1[there, :] + (1.0 - b2) * (g * g)
                w = stage[here, :] - lr * (m * ic1) / (jnp.sqrt(v * ic2) + eps)
                r1[here, :] = m
                r1[there, :] = v
                stage[here, :] = w
                mine[here, :] = w.astype(BF16)
                return 0
            lax.fori_loop(0, CH // 32, adam, 0)
            here = slot(k, i, 0)
            for step in range(3):
                send(mine_at(k, i), here, k, i, 0, step).start()
            across(mine_at(k, i), here, k, i, 0).start()
        return 0
    lax.fori_loop(0, 2, fifth, 0)
    keep = pltpu.make_async_copy(mine, out.at[pl.ds(pl.multiple_of(me * WR, 32), WR)], lsem.at[1])
    keep.start()

    ks = [(k, s) for s in range(2) for k in range(3)]

    def arrive(e, _):
        for k, s in ks:
            here = slot(k, s, e)
            send(here, here, k, s, e - 1, 0).wait_recv()
            for step in (1, 2):
                @pl.when(e < (1 << step))
                def _(k=k, s=s, here=here, step=step):
                    send(here, here, k, s, e, step).start()
            across(here, here, k, s, e).start()
        return 0

    for (_, dst, src, first), (lo, hi) in zip(state, ((1, 2), (2, 4), (4, 8))):
        to_flat_order(src, first, dst)
        lax.fori_loop(lo, hi, arrive, 0)

    def finish(i, _):
        any_chunk = mine_at(0, 0)

        def desc(ss, rs):
            return pltpu.make_async_remote_copy(any_chunk, any_chunk, ss.at[i], rs.at[i],
                                                device_id=peers[0], device_id_type=MESH)
        desc(asend, arecv).wait_recv()
        desc(asend, arecv).wait_send()

        @pl.when(i % 8 > 0)
        def _():
            desc(isend, irecv).wait_send()
        return 0
    lax.fori_loop(0, 48, finish, 0)
    keep.wait()

    def drain(i, _):
        for k in range(3):
            c = i * 3 + k

            @pl.when(i < 2)
            def _(k=k, c=c):
                hop(acc, c, r3, c, s3, q3, k, 2).wait_send()
            hop(acc, c, r2, c, s2, q2, k, 1).wait_send()
            hop(acc, 12 + c, r1, 12 + c, s1, q1, k, 0).wait_send()
        return 0
    lax.fori_loop(0, 4, drain, 0)

    def draind(c, _):
        d2d_desc(c).wait_send()
        return 0
    lax.fori_loop(0, 48, draind, 0)


ANY = pl.BlockSpec(memory_space=pl.ANY)


def step_call(scal, grads, m, v, w):
    dma = pltpu.SemaphoreType.DMA
    flat = jax.ShapeDtypeStruct((SHARD,), F32)
    return pl.pallas_call(
        step_kernel,
        out_shape=(jax.ShapeDtypeStruct((NDEV * WR, 128), BF16), flat, flat, flat),
        in_specs=[pl.BlockSpec(memory_space=pltpu.SMEM)] + [ANY] * 9,
        out_specs=[ANY] * 4,
        scratch_shapes=[
            pltpu.VMEM((48 * CH, 128), F32), pltpu.VMEM((24 * CH, 128), F32), pltpu.VMEM((12 * CH, 128), F32),
            pltpu.VMEM((6 * CH, 128), F32), pltpu.VMEM((NST * CH, 128), F32),
            pltpu.VMEM((SHARD,), F32), pltpu.VMEM((WR, 128), BF16),
            dma((48,)), dma((48,)), dma((NST,)), dma((24,)), dma((24,)), dma((12,)), dma((12,)), dma((6,)), dma((6,)),
            dma((2,)), dma((48,)), dma((48,)), dma((48,)), dma((48,)),
        ],
        compiler_params=pltpu.CompilerParams(collective_id=0, has_side_effects=True, vmem_limit_bytes=67043328),
        name="step",
    )(scal, *grads, m, v, w)


BSTART = [block_start(w) for w in range(NDEV)]


def put_kernel(slots, m, v, w, m_out, v_out, w_out, o0, o1, o2, o3, o4, o5, buf, mb, vb, wb, isem, osem):
    outs = (o0, o1, o2, o3, o4, o5)
    state = ((m, mb, m_out), (v, vb, v_out), (w, wb, w_out))
    loads = [pltpu.make_async_copy(slots.at[pl.ds(w * WR, WR)], buf.at[pl.ds(w * WR, WR)], isem.at[w])
             for w in range(NDEV)]
    loads += [pltpu.make_async_copy(a, b, isem.at[NDEV + i]) for i, (a, b, _) in enumerate(state)]
    for c in loads:
        c.start()
    stores = []
    for w in range(NDEV):
        loads[w].wait()
        t, n, _ = BSTART[w]
        bound = w * SHARD - t * 1024
        if bound > 0:
            a, b = win_start(w), win_start(w - 1)
            p = (lax.broadcasted_iota(jnp.int32, (8, 128), 0) * (n * 128)
                 + lax.broadcasted_iota(jnp.int32, (8, 128), 1))
            for j in range(n):
                if j * 128 < bound:
                    here = pl.ds(w * WR + (t + j - a) * 8, 8)
                    x = buf[here, :].astype(F32)
                    y = buf[pl.ds((w - 1) * WR + (t + j - b) * 8, 8), :].astype(F32)
                    buf[here, :] = jnp.where(p + j * 128 < bound, y, x).astype(BF16)
        end = BSTART[w + 1][0] if w + 1 < NDEV else TOFF[6]
        for k in range(6):
            lo, hi = max(t, TOFF[k]), min(end, TOFF[k + 1])
            if lo < hi:
                c = pltpu.make_async_copy(
                    buf.at[pl.ds(w * WR + (lo - win_start(w)) * 8, (hi - lo) * 8)],
                    outs[k].at[pl.ds((lo - TOFF[k]) * 8, (hi - lo) * 8)], osem.at[len(stores)])
                c.start()
                stores.append(c)
    for i, (_, b, o) in enumerate(state):
        loads[NDEV + i].wait()
        c = pltpu.make_async_copy(b, o, osem.at[len(stores)])
        c.start()
        stores.append(c)
    for c in stores:
        c.wait()


def put(slots, m, v, w):
    flat = jax.ShapeDtypeStruct((SHARD,), F32)
    return pl.pallas_call(
        put_kernel,
        out_shape=(flat,) * 3 + tuple(jax.ShapeDtypeStruct(((TOFF[k + 1] - TOFF[k]) * 8, 128), BF16) for k in range(6)),
        in_specs=[ANY] * 4,
        out_specs=[ANY] * 9,
        scratch_shapes=[pltpu.VMEM((NDEV * WR, 128), BF16)] + [pltpu.VMEM((SHARD,), F32)] * 3 + [
                        pltpu.SemaphoreType.DMA((NDEV + 3,)),
                        pltpu.SemaphoreType.DMA((32,))],
        compiler_params=pltpu.CompilerParams(vmem_limit_bytes=67043328),
        name="put",
    )(slots, m, v, w)


def to_tiles(x):
    r, c = x.shape
    return x.reshape(r // 8, 8, c // 128, 128).transpose(0, 2, 1, 3).reshape(r * c // 128, 128)


def from_tiles(x, r, c):
    return x.reshape(r // 8, c // 128, 8, 128).transpose(0, 2, 1, 3).reshape(r, c)


def solution(mesh):
    def body(g_emb, g_qkv, g_o, g_w1, g_w2, g_bqkv, g_b1, g_dvec, m, v, w, lr, beta1, beta2, eps, step):
        big = [to_tiles(x.reshape(rc)) for x, rc in zip((g_emb, g_qkv, g_o, g_w1, g_w2), BIG)]
        small = jnp.concatenate([g_bqkv.reshape(-1, 128), g_b1.reshape(-1, 128), g_dvec.reshape(-1, 128),
                                 jnp.zeros((SMALL_TILES * 8 - sum(SMALL) // 128, 128), F32)])
        t = step.astype(F32)
        scal = jnp.stack([lr, beta1, beta2, eps, 1.0 / (1.0 - beta1 ** t), 1.0 / (1.0 - beta2 ** t)])
        m_new, v_new, w_new, *outs = put(*step_call(scal, (*big, small), m, v, w))
        wbs = [from_tiles(o, *rc) for o, rc in zip(outs, BIG)]
        r = [0, SMALL[0] // 128, (SMALL[0] + SMALL[1]) // 128, sum(SMALL) // 128]
        s = outs[5]
        return (m_new, v_new, w_new, wbs[0], wbs[1][None], wbs[2][None], wbs[3][None], wbs[4][None],
                s[r[0]:r[1]].reshape(1, -1), s[r[1]:r[2]].reshape(1, -1), s[r[2]:r[3]].reshape(1, 6, 1024))

    g3 = P(AXES, None, None)
    g4 = P(AXES, None, None, None)
    flat = P(AXES)
    rep = P()
    in_specs = (g3, g4, g4, g4, g4, g3, g3, g4, flat, flat, flat, rep, rep, rep, rep, rep)
    out_specs = (flat, flat, flat, rep, rep, rep, rep, rep, rep, rep, rep)
    return jax.shard_map(body, mesh=mesh, in_specs=in_specs, out_specs=out_specs, check_vma=False)
```

profile of v0, /device:TPU:0, one launch (start us, length us, event | category | flops | bytes accessed | tf_op | source)
XLA Modules:
  0.0 330.0 jit_solution(14722105291521358514)
XLA Ops:
  4.1 0.6 stack.27.sc
  4.7 0.1 pad.3.clone
  4.7 0.7 reduce
  5.5 1.5 maximum_maximum_fusion.g5
  7.0 291.7 %step.1 = (bf16[113664,128]{1,0:T(8,128)(2,1)}, f32[885488]{0:T(1024)}, f32[885488]{0:T(1024)}, f32[885488]{0:T(1024)}) custom-call(f32[6]{0:T(128)} %stack.27.sc, f32[32768,128]{1,0:T(8,128)} %bitcast.75, f32[24576,128]{1,0:T(8,128)} %bitcast.76, f32[8192,128]{1,0:T(8,128)} %bitcast.79, f32[22528,128]{1,0:T(8,128)} %bitcast.77, f32[22528,128]{1,0:T(8,128)} %bitcast.78, ...), custom_call_target="tpu_custom_call" | custom-call | tf_op jit(solution)/shard_map/step/pallas_call | solution.py:400
  298.7 27.4 %put.1 = (f32[885488]{0:T(1024)}, f32[885488]{0:T(1024)}, f32[885488]{0:T(1024)}, bf16[32768,128]{1,0:T(8,128)(2,1)}, bf16[24576,128]{1,0:T(8,128)(2,1)}, /*inde...) custom-call(bf16[113664,128]{1,0:T(8,128)(2,1)} %get-tuple-element.24.s, ...), custom_call_target="tpu_custom_call" | custom-call | tf_op jit(solution)/shard_map/put/pallas_call | solution.py:463
  326.0 0.7 slice_bitcast_fusion
  326.7 0.6 copy.32
  327.3 0.7 slice_bitcast_fusion.1
  328.0 0.7 slice.11
  328.8 0.6 reshape.89
  329.4 0.6 copy.31
  (1 shorter events, 0.0 us)
where the time goes:
time: 331 us; the launch traced here: 330 us
  Pallas kernels  319 us (96%)
  local copies, waits for them, and re-layouts  4.65 us (1%)
  between operations  4.08 us (1%)
    pallas_call x1, Pallas kernels, step_call(): pl.pallas_call(step_kernel, out_shape=(jax.ShapeDtypeStruct((NDEV * WR, 1...  292 us
    pallas_call x1, Pallas kernels, put(): pl.pallas_call(put_kernel, out_shape=(flat,) * 3 + tuple((jax.ShapeDtypeS...  27.4 us

commit v1 on v0

--- a/solution.py
+++ b/solution.py
@@ -68,14 +68,50 @@
 TAIL = SHARD % BLK // 128
 LAST = SHARD % 128
 PAD = 200
+LROWS = 7424
 
 
 NST = 6
 
 
-def step_kernel(sc, g0, g1, g2, g3, g4, g5, m_in, v_in, w_in, out, m_out, v_out, w_out,
+def each_block(me, one):
+    start = me * SHARD
+    base = win_start(me)
+    for k in range(6):
+        n = PER[k]
+        e0 = start - TOFF[k] * 1024
+        lo = jnp.minimum(jnp.maximum(e0, 0) // (n * 1024), NBLK[k])
+        hi = jnp.minimum((jnp.maximum(e0 + SHARD, 0) + n * 1024 - 1) // (n * 1024), NBLK[k])
+        t0 = TOFF[k] - base
+
+        def body(b, _, t0=t0, n=n):
+            row = pl.multiple_of((t0 + b * n) * 8, 8)
+            if n == 22:
+                @pl.when(row + 8 * n <= WR)
+                def _():
+                    one(row, n, n)
+
+                @pl.when(row + 8 * n > WR)
+                def _():
+                    one(row, n, 8)
+            else:
+                one(row, n, n)
+            return 0
+        lax.fori_loop(lo, hi, body, 0)
+
+
+def pieces(one):
+    def body(i, _):
+        one(pl.multiple_of(i * (BLK // 128), 8), BLK // 128, 128, pl.multiple_of(i * BLK, BLK))
+        return 0
+    lax.fori_loop(0, NB, body, 0)
+    one(NB * BLK // 128, TAIL, 128, NB * BLK)
+    one(NB * BLK // 128 + TAIL, 1, LAST, NB * BLK + TAIL * 128)
+
+
+def rs_kernel(sc, g0, g1, g2, g3, g4, g5, m_in, v_in, w_in, wb_out, m_out, v_out, w_out,
                 acc, r1, r2, r3, stage, raw, mine,
-                dsend, drecv, own, s1, q1, s2, q2, s3, q3, lsem, isend, irecv, asend, arecv):
+                dsend, drecv, own, s1, q1, s2, q2, s3, q3, lsem, osem):
     grads = (g0, g1, g2, g3, g4, g5)
     me = my_id()
     delta = deltas(me)
@@ -196,37 +232,6 @@
     flat_rows = acc
     lane8 = lax.broadcasted_iota(jnp.int32, (8, 128), 1)
 
-    def each_block(one):
-        for k in range(6):
-            n = PER[k]
-            e0 = start - TOFF[k] * 1024
-            lo = jnp.minimum(jnp.maximum(e0, 0) // (n * 1024), NBLK[k])
-            hi = jnp.minimum((jnp.maximum(e0 + SHARD, 0) + n * 1024 - 1) // (n * 1024), NBLK[k])
-            t0 = TOFF[k] - base
-
-            def body(b, _, t0=t0, n=n):
-                row = pl.multiple_of((t0 + b * n) * 8, 8)
-                if n == 22:
-                    @pl.when(row + 8 * n <= WR)
-                    def _():
-                        one(row, n, n)
-
-                    @pl.when(row + 8 * n > WR)
-                    def _():
-                        one(row, n, 8)
-                else:
-                    one(row, n, n)
-                return 0
-            lax.fori_loop(lo, hi, body, 0)
-
-    def pieces(one):
-        def body(i, _):
-            one(pl.multiple_of(i * (BLK // 128), 8), BLK // 128, 128, pl.multiple_of(i * BLK, BLK))
-            return 0
-        lax.fori_loop(0, NB, body, 0)
-        one(NB * BLK // 128, TAIL, 128, NB * BLK)
-        one(NB * BLK // 128 + TAIL, 1, LAST, NB * BLK + TAIL * 128)
-
     def to_tile_order(src, dst, first):
         load = pltpu.make_async_copy(src, raw, lsem.at[0])
         load.start()
@@ -244,32 +249,15 @@
                 x = flat_rows[pl.ds(row + j - q + PAD, 8, stride=n), :]
                 y = flat_rows[pl.ds(row + j - q + PAD - 1, 8, stride=n), :]
                 dst[pl.ds(pl.multiple_of(first + row + 8 * j, 8), 8), :] = jnp.where(lane8 >= off, x, y)
-        each_block(block)
-
-    def to_flat_order(src, first, dst):
-        def block(row, n, todo):
-            for j in range(todo):
-                flat_rows[pl.ds(row + j, 8, stride=n), :] = src[pl.ds(pl.multiple_of(first + row + 8 * j, 8), 8), :]
-        each_block(block)
-        back = (128 - off) % 128
-
-        def shift(row, rows, cols, e):
-            lane = lax.broadcasted_iota(jnp.int32, (rows, 128), 1)
-            x = pltpu.roll(flat_rows[pl.ds(q + row, rows), :], back, 1)
-            y = pltpu.roll(flat_rows[pl.ds(q + row + 1, rows), :], back, 1)
-            raw[pl.ds(e, rows * cols)] = jnp.where(lane < 128 - off, x, y)[:, :cols].reshape(rows * cols)
-        pieces(shift)
-        store = pltpu.make_async_copy(raw, dst, lsem.at[0])
-        store.start()
-        store.wait()
+        each_block(me, block)
 
     def free1(i, _):
         for k in range(3):
             hop(acc, i * 3 + k, r1, i * 3 + k, s1, q1, k, 0).wait_send()
         return 0
     lax.fori_loop(0, 4, free1, 0)
-    state = ((m_in, m_out, r1, 0), (v_in, v_out, r1, WR), (w_in, w_out, stage, 0))
-    for src, _, dst, first in state:
+    state = ((m_in, r1, 0), (v_in, r1, WR), (w_in, stage, 0))
+    for src, dst, first in state:
         to_tile_order(src, dst, first)
 
     def third(i, _):
@@ -291,22 +279,12 @@
         return 0
     lax.fori_loop(0, 2, fourth, 0)
 
-    def slot(k, s, e):
-        d1, d2, d3 = COLORS[k]
-        w = me + (e % 2) * delta[d1] + (e // 2 % 2) * delta[d2] + (e // 4) * delta[d3]
-        return out.at[pl.ds(pl.multiple_of(w * WR + (2 * k + s) * CH, 32), CH)]
-
-    def mine_at(k, s):
-        return mine.at[pl.ds((2 * k + s) * CH, CH)]
-
-    def send(src, dst, k, s, e, step):
-        i = (k * 2 + s) * 8 + e + (1 << step)
-        return pltpu.make_async_remote_copy(src, dst, isend.at[i], irecv.at[i],
-                                            device_id=peers[COLORS[k][step]], device_id_type=MESH)
-
-    def across(src, dst, k, s, e):
-        i = (k * 2 + s) * 8 + e
-        return pltpu.make_async_remote_copy(src, dst, asend.at[i], arecv.at[i], device_id=peers[0], device_id_type=MESH)
+    def results(k, i):
+        p = (2 * k + i) * CH
+        return [pltpu.make_async_copy(src.at[pl.ds(pl.multiple_of(first + p, 32), CH)],
+                                      dst.at[pl.ds(pl.multiple_of(p, 32), CH)], osem.at[j * 6 + 2 * k + i])
+                for j, (src, first, dst) in enumerate(
+                    ((mine, 0, wb_out), (r1, 0, m_out), (r1, WR, v_out), (stage, 0, w_out)))]
 
     lr, b1, b2, eps, ic1, ic2 = (sc[i] for i in range(6))
 
@@ -331,16 +309,114 @@
                 mine[here, :] = w.astype(BF16)
                 return 0
             lax.fori_loop(0, CH // 32, adam, 0)
-            here = slot(k, i, 0)
-            for step in range(3):
-                send(mine_at(k, i), here, k, i, 0, step).start()
-            across(mine_at(k, i), here, k, i, 0).start()
+            for copy in results(k, i):
+                copy.start()
         return 0
     lax.fori_loop(0, 2, fifth, 0)
-    keep = pltpu.make_async_copy(mine, out.at[pl.ds(pl.multiple_of(me * WR, 32), WR)], lsem.at[1])
-    keep.start()
+
+    def drain(i, _):
+        for k in range(3):
+            c = i * 3 + k
+
+            @pl.when(i < 2)
+            def _(k=k, c=c):
+                hop(acc, c, r3, c, s3, q3, k, 2).wait_send()
+            hop(acc, c, r2, c, s2, q2, k, 1).wait_send()
+            hop(acc, 12 + c, r1, 12 + c, s1, q1, k, 0).wait_send()
+        return 0
+    lax.fori_loop(0, 4, drain, 0)
+
+    def draind(c, _):
+        d2d_desc(c).wait_send()
+        return 0
+    lax.fori_loop(0, 48, draind, 0)
+
+    def written(i, _):
+        for k in range(3):
+            for copy in results(k, i):
+                copy.wait()
+        return 0
+    lax.fori_loop(0, 2, written, 0)
+
+
+ANY = pl.BlockSpec(memory_space=pl.ANY)
+
+
+HBM = pl.BlockSpec(memory_space=pltpu.HBM)
+VMEM = pl.BlockSpec(memory_space=pltpu.VMEM)
+
+
+def reduce_and_update(scal, grads, m, v, w):
+    dma = pltpu.SemaphoreType.DMA
+    win = jax.ShapeDtypeStruct((WR, 128), F32)
+    return pl.pallas_call(
+        rs_kernel,
+        out_shape=(jax.ShapeDtypeStruct((WR, 128), BF16), win, win, win),
+        in_specs=[pl.BlockSpec(memory_space=pltpu.SMEM)] + [HBM] * 9,
+        out_specs=[HBM] * 4,
+        scratch_shapes=[
+            pltpu.VMEM((48 * CH, 128), F32), pltpu.VMEM((24 * CH, 128), F32), pltpu.VMEM((12 * CH, 128), F32),
+            pltpu.VMEM((6 * CH, 128), F32), pltpu.VMEM((NST * CH, 128), F32),
+            pltpu.VMEM((SHARD,), F32), pltpu.VMEM((WR, 128), BF16),
+            dma((48,)), dma((48,)), dma((NST,)), dma((24,)), dma((24,)), dma((12,)), dma((12,)), dma((6,)), dma((6,)),
+            dma((2,)), dma((24,)),
+        ],
+        compiler_params=pltpu.CompilerParams(collective_id=0, has_side_effects=True, vmem_limit_bytes=67043328),
+        name="rs",
+    )(scal, *grads, m, v, w)
+
+
+def ag_kernel(wb, m_in, v_in, w_in, m_out, v_out, w_out, out, mt, vt, wt, flat_rows, lsem, isend, irecv, asend, arecv):
+    me = my_id()
+    delta = deltas(me)
+    peers = [coords(me + x) for x in delta]
+    load = pltpu.make_async_copy(wb, out.at[pl.ds(pl.multiple_of(me * WR, 32), WR)], lsem.at[0])
+    load.start()
+    state = ((m_in, mt, m_out), (v_in, vt, v_out), (w_in, wt, w_out))
+    loads = [pltpu.make_async_copy(src, dst.at[pl.ds(0, WR)], lsem.at[1 + i]) for i, (src, dst, _) in enumerate(state)]
+    for c in loads:
+        c.start()
+    entry_barrier(peers)
+    load.wait()
+    start = me * SHARD
+    off = start % 128
+    q = (start - off) // 128 - 8 * win_start(me)
+
+    def to_flat_order(src, dst):
+        def block(row, n, todo):
+            for j in range(todo):
+                flat_rows[pl.ds(row + j, 8, stride=n), :] = src[pl.ds(pl.multiple_of(row + 8 * j, 8), 8), :]
+        each_block(me, block)
+        back = (128 - off) % 128
+
+        def shift(row, rows, cols, e):
+            lane = lax.broadcasted_iota(jnp.int32, (rows, 128), 1)
+            x = pltpu.roll(flat_rows[pl.ds(q + row, rows), :], back, 1)
+            y = pltpu.roll(flat_rows[pl.ds(q + row + 1, rows), :], back, 1)
+            dst[pl.ds(e, rows * cols)] = jnp.where(lane < 128 - off, x, y)[:, :cols].reshape(rows * cols)
+        pieces(shift)
+
+    def slot(k, s, e):
+        d1, d2, d3 = COLORS[k]
+        w = me + (e % 2) * delta[d1] + (e // 2 % 2) * delta[d2] + (e // 4) * delta[d3]
+        return out.at[pl.ds(pl.multiple_of(w * WR + (2 * k + s) * CH, 32), CH)]
+
+    def send(src, dst, k, s, e, step):
+        i = (k * 2 + s) * 8 + e + (1 << step)
+        return pltpu.make_async_remote_copy(src, dst, isend.at[i], irecv.at[i],
+                                            device_id=peers[COLORS[k][step]], device_id_type=MESH)
+
+    def across(src, dst, k, s, e):
+        i = (k * 2 + s) * 8 + e
+        return pltpu.make_async_remote_copy(src, dst, asend.at[i], arecv.at[i], device_id=peers[0], device_id_type=MESH)
 
     ks = [(k, s) for s in range(2) for k in range(3)]
+
+    for k, s in ks:
+        here = slot(k, s, 0)
+        for step in range(3):
+            send(here, here, k, s, 0, step).start()
+        across(here, here, k, s, 0).start()
 
     def arrive(e, _):
         for k, s in ks:
@@ -353,12 +429,13 @@
             across(here, here, k, s, e).start()
         return 0
 
-    for (_, dst, src, first), (lo, hi) in zip(state, ((1, 2), (2, 4), (4, 8))):
-        to_flat_order(src, first, dst)
+    for c, (_, src, dst), (lo, hi) in zip(loads, state, ((1, 2), (2, 4), (4, 8))):
+        c.wait()
+        to_flat_order(src, dst)
         lax.fori_loop(lo, hi, arrive, 0)
 
     def finish(i, _):
-        any_chunk = mine_at(0, 0)
+        any_chunk = out.at[pl.ds(0, CH)]
 
         def desc(ss, rs):
             return pltpu.make_async_remote_copy(any_chunk, any_chunk, ss.at[i], rs.at[i],
@@ -371,106 +448,70 @@
             desc(isend, irecv).wait_send()
         return 0
     lax.fori_loop(0, 48, finish, 0)
-    keep.wait()
-
-    def drain(i, _):
-        for k in range(3):
-            c = i * 3 + k
-
-            @pl.when(i < 2)
-            def _(k=k, c=c):
-                hop(acc, c, r3, c, s3, q3, k, 2).wait_send()
-            hop(acc, c, r2, c, s2, q2, k, 1).wait_send()
-            hop(acc, 12 + c, r1, 12 + c, s1, q1, k, 0).wait_send()
-        return 0
-    lax.fori_loop(0, 4, drain, 0)
-
-    def draind(c, _):
-        d2d_desc(c).wait_send()
-        return 0
-    lax.fori_loop(0, 48, draind, 0)
-
-
-ANY = pl.BlockSpec(memory_space=pl.ANY)
-
-
-def step_call(scal, grads, m, v, w):
+
+
+def all_gather(wb, m, v, w):
     dma = pltpu.SemaphoreType.DMA
     flat = jax.ShapeDtypeStruct((SHARD,), F32)
     return pl.pallas_call(
-        step_kernel,
-        out_shape=(jax.ShapeDtypeStruct((NDEV * WR, 128), BF16), flat, flat, flat),
-        in_specs=[pl.BlockSpec(memory_space=pltpu.SMEM)] + [ANY] * 9,
-        out_specs=[ANY] * 4,
-        scratch_shapes=[
-            pltpu.VMEM((48 * CH, 128), F32), pltpu.VMEM((24 * CH, 128), F32), pltpu.VMEM((12 * CH, 128), F32),
-            pltpu.VMEM((6 * CH, 128), F32), pltpu.VMEM((NST * CH, 128), F32),
-            pltpu.VMEM((SHARD,), F32), pltpu.VMEM((WR, 128), BF16),
-            dma((48,)), dma((48,)), dma((NST,)), dma((24,)), dma((24,)), dma((12,)), dma((12,)), dma((6,)), dma((6,)),
-            dma((2,)), dma((48,)), dma((48,)), dma((48,)), dma((48,)),
-        ],
-        compiler_params=pltpu.CompilerParams(collective_id=0, has_side_effects=True, vmem_limit_bytes=67043328),
-        name="step",
-    )(scal, *grads, m, v, w)
+        ag_kernel,
+        out_shape=(flat, flat, flat, jax.ShapeDtypeStruct((NDEV * WR, 128), BF16)),
+        in_specs=[HBM] * 4,
+        out_specs=[VMEM, VMEM, VMEM, ANY],
+        scratch_shapes=[pltpu.VMEM((LROWS, 128), F32)] * 4 + [dma((4,)), dma((48,)), dma((48,)), dma((48,)), dma((48,))],
+        compiler_params=pltpu.CompilerParams(collective_id=1, has_side_effects=True, vmem_limit_bytes=16 << 20),
+        name="ag",
+    )(*(pltpu.with_memory_space_constraint(x, pltpu.HBM) for x in (wb, m, v, w)))
 
 
 BSTART = [block_start(w) for w in range(NDEV)]
 
 
-def put_kernel(slots, m, v, w, m_out, v_out, w_out, o0, o1, o2, o3, o4, o5, buf, mb, vb, wb, isem, osem):
+def put_kernel(slots, o0, o1, o2, o3, o4, o5, tmp, osem):
     outs = (o0, o1, o2, o3, o4, o5)
-    state = ((m, mb, m_out), (v, vb, v_out), (w, wb, w_out))
-    loads = [pltpu.make_async_copy(slots.at[pl.ds(w * WR, WR)], buf.at[pl.ds(w * WR, WR)], isem.at[w])
-             for w in range(NDEV)]
-    loads += [pltpu.make_async_copy(a, b, isem.at[NDEV + i]) for i, (a, b, _) in enumerate(state)]
-    for c in loads:
-        c.start()
     stores = []
-    for w in range(NDEV):
-        loads[w].wait()
-        t, n, _ = BSTART[w]
-        bound = w * SHARD - t * 1024
-        if bound > 0:
-            a, b = win_start(w), win_start(w - 1)
-            p = (lax.broadcasted_iota(jnp.int32, (8, 128), 0) * (n * 128)
-                 + lax.broadcasted_iota(jnp.int32, (8, 128), 1))
-            for j in range(n):
-                if j * 128 < bound:
-                    here = pl.ds(w * WR + (t + j - a) * 8, 8)
-                    x = buf[here, :].astype(F32)
-                    y = buf[pl.ds((w - 1) * WR + (t + j - b) * 8, 8), :].astype(F32)
-                    buf[here, :] = jnp.where(p + j * 128 < bound, y, x).astype(BF16)
-        end = BSTART[w + 1][0] if w + 1 < NDEV else TOFF[6]
-        for k in range(6):
-            lo, hi = max(t, TOFF[k]), min(end, TOFF[k + 1])
-            if lo < hi:
-                c = pltpu.make_async_copy(
-                    buf.at[pl.ds(w * WR + (lo - win_start(w)) * 8, (hi - lo) * 8)],
-                    outs[k].at[pl.ds((lo - TOFF[k]) * 8, (hi - lo) * 8)], osem.at[len(stores)])
-                c.start()
-                stores.append(c)
-    for i, (_, b, o) in enumerate(state):
-        loads[NDEV + i].wait()
-        c = pltpu.make_async_copy(b, o, osem.at[len(stores)])
+
+    def store(src, dst):
+        c = pltpu.make_async_copy(src, dst, osem.at[len(stores)])
         c.start()
         stores.append(c)
+
+    def store_tiles(ref, row, lo, hi):
+        for k in range(6):
+            a, b = max(lo, TOFF[k]), min(hi, TOFF[k + 1])
+            if a < b:
+                store(ref.at[pl.ds(row + (a - lo) * 8, (b - a) * 8)], outs[k].at[pl.ds((a - TOFF[k]) * 8, (b - a) * 8)])
+
+    for d in range(NDEV):
+        t, n, _ = BSTART[d]
+        lo = t + n if d else 0
+        store_tiles(slots, d * WR + (lo - win_start(d)) * 8, lo, BSTART[d + 1][0] if d + 1 < NDEV else TOFF[6])
+    for d in range(1, NDEV):
+        t, n, _ = BSTART[d]
+        bound = d * SHARD - t * 1024
+        p = (lax.broadcasted_iota(jnp.int32, (8, 128), 0) * (n * 128)
+             + lax.broadcasted_iota(jnp.int32, (8, 128), 1))
+        for j in range(n):
+            x = slots[pl.ds(d * WR + (t + j - win_start(d)) * 8, 8), :]
+            if j * 128 < bound:
+                y = slots[pl.ds((d - 1) * WR + (t + j - win_start(d - 1)) * 8, 8), :]
+                x = jnp.where(p + j * 128 < bound, y.astype(F32), x.astype(F32)).astype(BF16)
+            tmp[pl.ds(d * 192 + j * 8, 8), :] = x
+        store_tiles(tmp, d * 192, t, t + n)
     for c in stores:
         c.wait()
 
 
-def put(slots, m, v, w):
-    flat = jax.ShapeDtypeStruct((SHARD,), F32)
+def put(slots):
     return pl.pallas_call(
         put_kernel,
-        out_shape=(flat,) * 3 + tuple(jax.ShapeDtypeStruct(((TOFF[k + 1] - TOFF[k]) * 8, 128), BF16) for k in range(6)),
-        in_specs=[ANY] * 4,
-        out_specs=[ANY] * 9,
-        scratch_shapes=[pltpu.VMEM((NDEV * WR, 128), BF16)] + [pltpu.VMEM((SHARD,), F32)] * 3 + [
-                        pltpu.SemaphoreType.DMA((NDEV + 3,)),
-                        pltpu.SemaphoreType.DMA((32,))],
-        compiler_params=pltpu.CompilerParams(vmem_limit_bytes=67043328),
+        out_shape=tuple(jax.ShapeDtypeStruct(((TOFF[k + 1] - TOFF[k]) * 8, 128), BF16) for k in range(6)),
+        in_specs=[VMEM],
+        out_specs=[HBM] * 6,
+        scratch_shapes=[pltpu.VMEM((NDEV * 192, 128), BF16), pltpu.SemaphoreType.DMA((48,))],
+        compiler_params=pltpu.CompilerParams(vmem_limit_bytes=4 << 20),
         name="put",
-    )(slots, m, v, w)
+    )(slots)
 
 
 def to_tiles(x):
@@ -489,7 +530,8 @@
                                  jnp.zeros((SMALL_TILES * 8 - sum(SMALL) // 128, 128), F32)])
         t = step.astype(F32)
         scal = jnp.stack([lr, beta1, beta2, eps, 1.0 / (1.0 - beta1 ** t), 1.0 / (1.0 - beta2 ** t)])
-        m_new, v_new, w_new, *outs = put(*step_call(scal, (*big, small), m, v, w))
+        m_new, v_new, w_new, slots = all_gather(*reduce_and_update(scal, (*big, small), m, v, w))
+        outs = put(slots)
         wbs = [from_tiles(o, *rc) for o, rc in zip(outs, BIG)]
         r = [0, SMALL[0] // 128, (SMALL[0] + SMALL[1]) // 128, sum(SMALL) // 128]
         s = outs[5]

time: 331 us -> 328 us (level)
  Pallas kernels: 319 us -> 308 us
  local copies, waits for them, and re-layouts: 4.65 us -> 13.6 us
    pallas_call x2 -> x3, Pallas kernels: 319 us -> 308 us  [the longest x1 198 us: reduce_and_update(): pl.pallas_call(rs_kernel, out_shape=(jax.ShapeDtypeStruct((WR, 128), BF16...]
    unnamed x4 -> x13, local copies, waits for them, and re-layouts: 2.61 us -> 12.3 us
where the time goes in v1:
time: 328 us
  Pallas kernels  308 us (94%)
  local copies, waits for them, and re-layouts  13.6 us (4%)
  between operations  4.11 us (1%)
    pallas_call x1, Pallas kernels, reduce_and_update(): pl.pallas_call(rs_kernel, out_shape=(jax.ShapeDtypeStruct((WR, 128), BF16...  198 us
    pallas_call x1, Pallas kernels, all_gather(): pl.pallas_call(ag_kernel, out_shape=(flat, flat, flat, jax.ShapeDtypeStru...  99.9 us
    unnamed x13, local copies, waits for them, and re-layouts  12.3 us
    pallas_call x1, Pallas kernels, put(): pl.pallas_call(put_kernel, out_shape=tuple((jax.ShapeDtypeStruct(((TOFF[k...  9.89 us

profile of v1, /device:TPU:0, one launch (start us, length us, event | category | flops | bytes accessed | tf_op | source)
XLA Modules:
  0.0 327.9 jit_solution(16172870894731022619)
XLA Ops:
  4.1 0.6 stack.27.sc
  4.7 0.1 pad.3.clone
  4.7 0.7 reduce
  5.5 1.5 maximum_maximum_fusion.g5
  7.0 198.1 %rs.1 = (bf16[7104,128]{1,0:T(8,128)(2,1)}, f32[7104,128]{1,0:T(8,128)}, f32[7104,128]{1,0:T(8,128)}, f32[7104,128]{1,0:T(8,128)}) custom-call(f32[6]{0:T(128)} %stack.27.sc, f32[32768,128]{1,0:T(8,128)} %bitcast.75, f32[24576,128]{1,0:T(8,128)} %bitcast.76, f32[8192,128]{1,0:T(8,128)} %bitcast.79, f32[22528,128]{1,0:T(8,128)} %bitcast.77, ...), custom_call_target="tpu_custom_call" | custom-call | tf_op jit(solution)/shard_map/rs/pallas_call | solution.py:352
  205.1 99.9 %ag.1 = (f32[885488]{0:T(1024)S(1)}, f32[885488]{0:T(1024)S(1)}, f32[885488]{0:T(1024)S(1)}, bf16[113664,128]{1,0:T(8,128)(2,1)S(1)}) custom-call(bf16[7104,128]{1,0:T(8,128)(2,1)} %get-tuple-element.25.wb, f32[7104,128]{1,0:T(8,128)} %get-tuple-element.26.m_in, f32[7104,128]{1,0:T(8,128)} %get-tuple-element.27.v_in, f32[7104,128]{1,0:T(8,128)} %get-tuple-element.28.w_in), custom_call_target="tpu_custom_call" | custom-call | tf_op jit(solution)/shard_map/ag/pallas_call | solution.py:456
  305.0 0.0 copy-start
  305.1 0.0 copy-start.2
  305.1 9.9 %put.1 = (bf16[32768,128]{1,0:T(8,128)(2,1)}, bf16[24576,128]{1,0:T(8,128)(2,1)}, bf16[8192,128]{1,0:T(8,128)(2,1)}, bf16[22528,128]{1,0:T(8,128)(2,1)}, bf16[22...) custom-call(bf16[113664,128]{1,0:T(8,128)(2,1)S(1)} %get-tuple-element.32.slots), custom_call_target="tpu_custom_call" | custom-call | tf_op jit(solution)/shard_map/put/pallas_call | solution.py:506
  315.0 0.4 copy-done
  315.3 1.2 copy-done.2
  316.5 0.6 copy.32
  317.1 0.6 slice_bitcast_fusion.1
  317.7 0.6 reshape.89
  318.4 0.0 copy-start.1
  318.4 1.4 copy.31
  319.8 4.0 %copy.41 = f32[885488]{0:T(1024)} copy(f32[885488]{0:T(1024)} %copy-done.2) | data formatting | bytes 7083904
  323.9 0.0 copy-done.1
  323.9 2.0 copy.42
  325.9 2.0 copy.43
  (3 shorter events, 0.0 us)
Async XLA Ops:
  305.0 10.3 %copy-start = (f32[885488]{0:T(1024)}, f32[885488]{0:T(1024)S(1)}, u32[]{:S(2)}) copy-start(f32[885488]{0:T(1024)S(1)} %get-tuple-element.51) | copy-start | bytes 10625860
  305.1 11.5 %copy-start.2 = (f32[885488]{0:T(1024)}, f32[885488]{0:T(1024)S(1)}, u32[]{:S(2)}) copy-start(f32[885488]{0:T(1024)S(1)} %get-tuple-element.50) | copy-start | bytes 10625860
  318.4 5.5 %copy-start.1 = (f32[885488]{0:T(1024)S(1)}, f32[885488]{0:T(1024)}, u32[]{:S(2)}) copy-start(f32[885488]{0:T(1024)} %copy-done) | copy-start | bytes 10625860

commit v2 on v1

--- a/solution.py
+++ b/solution.py
@@ -68,6 +68,8 @@
 TAIL = SHARD % BLK // 128
 LAST = SHARD % 128
 PAD = 200
+FSTEP = 32
+FROWS = 6944
 LROWS = 7424
 
 
@@ -366,14 +368,14 @@
     )(scal, *grads, m, v, w)
 
 
-def ag_kernel(wb, m_in, v_in, w_in, m_out, v_out, w_out, out, mt, vt, wt, flat_rows, lsem, isend, irecv, asend, arecv):
+def ag_kernel(wb, m_in, v_in, w_in, flat, out, mt, vt, wt, flat_rows, lsem, isend, irecv, asend, arecv):
     me = my_id()
     delta = deltas(me)
     peers = [coords(me + x) for x in delta]
     load = pltpu.make_async_copy(wb, out.at[pl.ds(pl.multiple_of(me * WR, 32), WR)], lsem.at[0])
     load.start()
-    state = ((m_in, mt, m_out), (v_in, vt, v_out), (w_in, wt, w_out))
-    loads = [pltpu.make_async_copy(src, dst.at[pl.ds(0, WR)], lsem.at[1 + i]) for i, (src, dst, _) in enumerate(state)]
+    state = ((m_in, mt), (v_in, vt), (w_in, wt))
+    loads = [pltpu.make_async_copy(src, dst.at[pl.ds(0, WR)], lsem.at[1 + i]) for i, (src, dst) in enumerate(state)]
     for c in loads:
         c.start()
     entry_barrier(peers)
@@ -382,19 +384,21 @@
     off = start % 128
     q = (start - off) // 128 - 8 * win_start(me)
 
-    def to_flat_order(src, dst):
+    def to_flat_order(src, first):
         def block(row, n, todo):
             for j in range(todo):
                 flat_rows[pl.ds(row + j, 8, stride=n), :] = src[pl.ds(pl.multiple_of(row + 8 * j, 8), 8), :]
         each_block(me, block)
         back = (128 - off) % 128
-
-        def shift(row, rows, cols, e):
-            lane = lax.broadcasted_iota(jnp.int32, (rows, 128), 1)
-            x = pltpu.roll(flat_rows[pl.ds(q + row, rows), :], back, 1)
-            y = pltpu.roll(flat_rows[pl.ds(q + row + 1, rows), :], back, 1)
-            dst[pl.ds(e, rows * cols)] = jnp.where(lane < 128 - off, x, y)[:, :cols].reshape(rows * cols)
-        pieces(shift)
+        lane = lax.broadcasted_iota(jnp.int32, (FSTEP, 128), 1)
+
+        def shift(i, _):
+            row = pl.multiple_of(i * FSTEP, 8)
+            x = pltpu.roll(flat_rows[pl.ds(q + row, FSTEP), :], back, 1)
+            y = pltpu.roll(flat_rows[pl.ds(q + row + 1, FSTEP), :], back, 1)
+            flat[pl.ds(pl.multiple_of(first + row, 8), FSTEP), :] = jnp.where(lane < 128 - off, x, y)
+            return 0
+        lax.fori_loop(0, FROWS // FSTEP, shift, 0)
 
     def slot(k, s, e):
         d1, d2, d3 = COLORS[k]
@@ -429,9 +433,9 @@
             across(here, here, k, s, e).start()
         return 0
 
-    for c, (_, src, dst), (lo, hi) in zip(loads, state, ((1, 2), (2, 4), (4, 8))):
-        c.wait()
-        to_flat_order(src, dst)
+    for i, (lo, hi) in enumerate(((1, 2), (2, 4), (4, 8))):
+        loads[i].wait()
+        to_flat_order(state[i][1], i * FROWS)
         lax.fori_loop(lo, hi, arrive, 0)
 
     def finish(i, _):
@@ -452,12 +456,11 @@
 
 def all_gather(wb, m, v, w):
     dma = pltpu.SemaphoreType.DMA
-    flat = jax.ShapeDtypeStruct((SHARD,), F32)
     return pl.pallas_call(
         ag_kernel,
-        out_shape=(flat, flat, flat, jax.ShapeDtypeStruct((NDEV * WR, 128), BF16)),
+        out_shape=(jax.ShapeDtypeStruct((3 * FROWS, 128), F32), jax.ShapeDtypeStruct((NDEV * WR, 128), BF16)),
         in_specs=[HBM] * 4,
-        out_specs=[VMEM, VMEM, VMEM, ANY],
+        out_specs=[VMEM, ANY],
         scratch_shapes=[pltpu.VMEM((LROWS, 128), F32)] * 4 + [dma((4,)), dma((48,)), dma((48,)), dma((48,)), dma((48,))],
         compiler_params=pltpu.CompilerParams(collective_id=1, has_side_effects=True, vmem_limit_bytes=16 << 20),
         name="ag",
@@ -467,8 +470,8 @@
 BSTART = [block_start(w) for w in range(NDEV)]
 
 
-def put_kernel(slots, o0, o1, o2, o3, o4, o5, tmp, osem):
-    outs = (o0, o1, o2, o3, o4, o5)
+def put_kernel(state, slots, m_out, v_out, w_out, o0, o1, o2, o3, o4, o_bqkv, o_b1, o_dvec, tmp, mb, vb, wb, osem):
+    outs = (o0, o1, o2, o3, o4)
     stores = []
 
     def store(src, dst):
@@ -477,7 +480,7 @@
         stores.append(c)
 
     def store_tiles(ref, row, lo, hi):
-        for k in range(6):
+        for k in range(5):
             a, b = max(lo, TOFF[k]), min(hi, TOFF[k + 1])
             if a < b:
                 store(ref.at[pl.ds(row + (a - lo) * 8, (b - a) * 8)], outs[k].at[pl.ds((a - TOFF[k]) * 8, (b - a) * 8)])
@@ -498,20 +501,38 @@
                 x = jnp.where(p + j * 128 < bound, y.astype(F32), x.astype(F32)).astype(BF16)
             tmp[pl.ds(d * 192 + j * 8, 8), :] = x
         store_tiles(tmp, d * 192, t, t + n)
+    at = (NDEV - 1) * WR + (TOFF[5] - win_start(NDEV - 1)) * 8
+    rows = slots[pl.ds(at, 96), :].astype(F32)
+    for j in range(24):
+        o_bqkv[:, j * 128:(j + 1) * 128] = rows[j:j + 1].astype(BF16)
+    for j in range(22):
+        o_b1[:, j * 128:(j + 1) * 128] = rows[24 + j:25 + j].astype(BF16)
+    for i in range(6):
+        for j in range(8):
+            o_dvec[0, i:i + 1, j * 128:(j + 1) * 128] = rows[46 + 8 * i + j:47 + 8 * i + j].astype(BF16)
+    for i, (buf, out) in enumerate(((mb, m_out), (vb, v_out), (wb, w_out))):
+        def cut(row, rows, cols, e, i=i, buf=buf):
+            buf[pl.ds(e, rows * cols)] = state[pl.ds(i * FROWS + row, rows), :][:, :cols].reshape(rows * cols)
+        pieces(cut)
+        store(buf, out)
     for c in stores:
         c.wait()
 
 
-def put(slots):
+def put(state, slots):
+    flat = jax.ShapeDtypeStruct((SHARD,), F32)
     return pl.pallas_call(
         put_kernel,
-        out_shape=tuple(jax.ShapeDtypeStruct(((TOFF[k + 1] - TOFF[k]) * 8, 128), BF16) for k in range(6)),
-        in_specs=[VMEM],
-        out_specs=[HBM] * 6,
-        scratch_shapes=[pltpu.VMEM((NDEV * 192, 128), BF16), pltpu.SemaphoreType.DMA((48,))],
-        compiler_params=pltpu.CompilerParams(vmem_limit_bytes=4 << 20),
+        out_shape=(flat,) * 3 + tuple(jax.ShapeDtypeStruct(((TOFF[k + 1] - TOFF[k]) * 8, 128), BF16) for k in range(5)) + (
+            jax.ShapeDtypeStruct((1, SMALL[0]), BF16), jax.ShapeDtypeStruct((1, SMALL[1]), BF16),
+            jax.ShapeDtypeStruct((1, 6, 1024), BF16)),
+        in_specs=[VMEM] * 2,
+        out_specs=[HBM] * 8 + [VMEM] * 3,
+        scratch_shapes=[pltpu.VMEM((NDEV * 192, 128), BF16)] + [pltpu.VMEM((SHARD,), F32)] * 3 + [
+            pltpu.SemaphoreType.DMA((48,))],
+        compiler_params=pltpu.CompilerParams(vmem_limit_bytes=16 << 20),
         name="put",
-    )(slots)
+    )(state, slots)
 
 
 def to_tiles(x):
@@ -530,13 +551,9 @@
                                  jnp.zeros((SMALL_TILES * 8 - sum(SMALL) // 128, 128), F32)])
         t = step.astype(F32)
         scal = jnp.stack([lr, beta1, beta2, eps, 1.0 / (1.0 - beta1 ** t), 1.0 / (1.0 - beta2 ** t)])
-        m_new, v_new, w_new, slots = all_gather(*reduce_and_update(scal, (*big, small), m, v, w))
-        outs = put(slots)
+        m_new, v_new, w_new, *outs = put(*all_gather(*reduce_and_update(scal, (*big, small), m, v, w)))
         wbs = [from_tiles(o, *rc) for o, rc in zip(outs, BIG)]
-        r = [0, SMALL[0] // 128, (SMALL[0] + SMALL[1]) // 128, sum(SMALL) // 128]
-        s = outs[5]
-        return (m_new, v_new, w_new, wbs[0], wbs[1][None], wbs[2][None], wbs[3][None], wbs[4][None],
-                s[r[0]:r[1]].reshape(1, -1), s[r[1]:r[2]].reshape(1, -1), s[r[2]:r[3]].reshape(1, 6, 1024))
+        return (m_new, v_new, w_new, wbs[0], wbs[1][None], wbs[2][None], wbs[3][None], wbs[4][None], *outs[5:])
 
     g3 = P(AXES, None, None)
     g4 = P(AXES, None, None, None)

time: 328 us -> 319 us (0.973)
  local copies, waits for them, and re-layouts: 13.6 us -> 0.68 us
  Pallas kernels: 308 us -> 312 us
    unnamed x13 -> x0, local copies, waits for them, and re-layouts: 12.3 us -> none
    pallas_call x2, Pallas kernels: 110 us -> 114 us  [the longest x1 100 us: all_gather(): pl.pallas_call(ag_kernel, out_shape=(jax.ShapeDtypeStruct((3 * FROWS, 128...]
where the time goes in v2:
time: 319 us
  Pallas kernels  312 us (98%)
  between operations  4.08 us (1%)
    pallas_call x1, Pallas kernels, reduce_and_update(): pl.pallas_call(rs_kernel, out_shape=(jax.ShapeDtypeStruct((WR, 128), BF16...  198 us
    pallas_call x1, Pallas kernels, all_gather(): pl.pallas_call(ag_kernel, out_shape=(jax.ShapeDtypeStruct((3 * FROWS, 128...  100 us
    pallas_call x1, Pallas kernels, put(): pl.pallas_call(put_kernel, out_shape=(flat,) * 3 + tuple((jax.ShapeDtypeS...  13.6 us

profile of v2, /device:TPU:0, one launch (start us, length us, event | category | flops | bytes accessed | tf_op | source)
XLA Modules:
  0.0 318.8 jit_solution(4835179745730079239)
XLA Ops:
  4.1 0.6 stack.27.sc
  4.7 0.1 pad.3.clone
  4.7 0.7 reduce
  5.5 1.5 maximum_maximum_fusion.g5
  7.0 198.1 %rs.1 = (bf16[7104,128]{1,0:T(8,128)(2,1)}, f32[7104,128]{1,0:T(8,128)}, f32[7104,128]{1,0:T(8,128)}, f32[7104,128]{1,0:T(8,128)}) custom-call(f32[6]{0:T(128)} %stack.27.sc, f32[32768,128]{1,0:T(8,128)} %bitcast.63, f32[24576,128]{1,0:T(8,128)} %bitcast.64, f32[8192,128]{1,0:T(8,128)} %bitcast.67, f32[22528,128]{1,0:T(8,128)} %bitcast.65, ...), custom_call_target="tpu_custom_call" | custom-call | tf_op jit(solution)/shard_map/rs/pallas_call | solution.py:354
  205.1 100.0 %ag.1 = (f32[20832,128]{1,0:T(8,128)S(1)}, bf16[113664,128]{1,0:T(8,128)(2,1)S(1)}) custom-call(bf16[7104,128]{1,0:T(8,128)(2,1)} %get-tuple-element.28.wb, f32[7104,128]{1,0:T(8,128)} %get-tuple-element.29.m_in, f32[7104,128]{1,0:T(8,128)} %get-tuple-element.30.v_in, f32[7104,128]{1,0:T(8,128)} %get-tuple-element.31.w_in), custom_call_target="tpu_custom_call" | custom-call | tf_op jit(solution)/shard_map/ag/pallas_call | solution.py:459
  305.1 13.6 %put.1 = (f32[885488]{0:T(1024)}, f32[885488]{0:T(1024)}, f32[885488]{0:T(1024)}, bf16[32768,128]{1,0:T(8,128)(2,1)}, bf16[24576,128]{1,0:T(8,128)(2,1)}, /*inde...) custom-call(f32[20832,128]{1,0:T(8,128)S(1)} %get-tuple-element.32.s, ...), custom_call_target="tpu_custom_call" | custom-call | tf_op jit(solution)/shard_map/put/pallas_call | solution.py:524
  (1 shorter events, 0.0 us)
